TPU v7x, 32 devices: a whole 2x2x4 slice. The times are simulated.
32 devices in a mesh: horiz: 8 (over y, x, core), lev: 4 (over z).
Axes of the slice: x: 2, y: 2, z: 4, core: 2. Of those that a mesh axis runs over, the one named last changes fastest.
Arguments:
- source_state: bfloat16 [5, 68, 32768], P(None, 'lev', 'horiz'), may hold values from -6 to 6
- intersection: int32 [40], P('horiz'), may hold values from 0 to 7, as said below
- index_map: int32 [40, 512], P('horiz'), may hold values from 0 to 4095
- blocks: bfloat16 [40, 512, 2048], P('horiz'), may hold values from -0.125 to 0.125
- bracket: int32 [127, 16384], P(None, ('horiz', 'lev')), may hold values from 0 to 66
- fraction: float32 [127, 16384], P(None, ('horiz', 'lev')), may hold values from 0 to 1
Outputs:
- target_state: bfloat16 [5, 127, 16384], P(None, None, ('horiz', 'lev'))
Inputs may be any that keep to these rules, and one draw needn't show every extreme that they name: For every target group g, intersection[g * 5] to intersection[g * 5 + 4] are the groups g - 2 to g + 2 modulo 8, each once, in some order.
All inputs are finite; a program needn't handle non-finite values.
Results may differ from a plain program's by a relative error of at most 0.0049.
Values may be sent and summed in bfloat16 or wider, within the bound.
A program may use at most 64 MiB of HBM per device.

v0:
```python
import jax
import jax.numpy as jnp
from jax import lax
from jax.sharding import PartitionSpec as P


def shifted(block, axis, distance):
    devices = range(lax.axis_size(axis))
    route = [((i - distance) % len(devices), i) for i in devices]
    return lax.ppermute(block, axis, route)


def select_cells(tile, wanted):
    cell_ids = jnp.arange(tile.shape[1], dtype=jnp.int32)[:, None]
    picker = (cell_ids == wanted[None, :]).astype(jnp.bfloat16)
    return jnp.dot(tile, picker, preferred_element_type=jnp.float32).astype(jnp.bfloat16)


def local(source_state, intersection, index_map, blocks, bracket, fraction):
    fields, level_slab, tile_cells = source_state.shape
    stacked = source_state.reshape(fields * level_slab, tile_cells)
    groups = lax.axis_size("horiz")
    block_count = intersection.shape[0]
    depth = (block_count - 1) // 2
    own_group = lax.axis_index("horiz")
    position = (intersection - own_group + depth) % groups
    collected = []
    for offset in range(-depth, depth + 1):
        wanted_group = (own_group + offset) % groups
        matched = intersection == wanted_group
        request = jnp.sum(jnp.where(matched[:, None], index_map, 0), axis=0)
        if offset == 0:
            collected.append(select_cells(stacked, request))
        else:
            incoming = shifted(request, "horiz", offset)
            outgoing = select_cells(stacked, incoming)
            collected.append(shifted(outgoing, "horiz", -offset))
    by_offset = jnp.stack(collected)
    pieces = [
        lax.dynamic_index_in_dim(by_offset, position[block_slot], 0, keepdims=False)
        for block_slot in range(block_count)
    ]
    chosen = jnp.concatenate(pieces, axis=1)
    weights_flat = blocks.reshape(-1, blocks.shape[2])
    horizontal = jnp.dot(chosen, weights_flat, preferred_element_type=jnp.float32).astype(
        jnp.bfloat16
    )
    horizontal = horizontal.reshape(fields, level_slab, blocks.shape[2])
    level_total = level_slab * lax.axis_size("lev")
    level_ids = jnp.arange(level_total, dtype=jnp.int32)[None, :, None]
    lower_hit = level_ids == bracket[:, None, :]
    upper_hit = level_ids == bracket[:, None, :] + 1
    upper_share = fraction[:, None, :]
    interp = jnp.where(lower_hit, 1.0 - upper_share, 0.0) + jnp.where(upper_hit, upper_share, 0.0)
    widened = lax.all_to_all(horizontal, "lev", split_axis=2, concat_axis=1, tiled=True).astype(
        jnp.float32
    )
    mixed = jnp.einsum("jlc,flc->fjc", interp, widened, precision=lax.Precision.HIGHEST)
    return mixed.astype(jnp.bfloat16)


def solution(mesh):
    in_specs = (
        P(None, "lev", "horiz"),
        P("horiz"),
        P("horiz", None),
        P("horiz", None, None),
        P(None, ("horiz", "lev")),
        P(None, ("horiz", "lev")),
    )
    out_specs = P(None, None, ("horiz", "lev"))
    return jax.shard_map(local, mesh=mesh, in_specs=in_specs, out_specs=out_specs, check_vma=False)
```

profile of v0, /device:TPU:2, one launch (start us, length us, event | category | flops | bytes accessed | tf_op | source)
XLA Modules:
  0.0 84.0 jit_solution(5691113030933345913)
XLA Ops:
  0.7 0.8 select_reduce_fusion
  1.6 2.4 %collective-permute-start = (s32[512]{0:T(512)S(1)}, s32[512]{0:T(512)S(1)}, u32[]{:S(2)}, u32[]{:S(2)}) collective-permute-start(s32[512]{0:T(512)S(1)} %get-tuple-element.8), channel_id=1, source_target_pairs={{8,0},{12,4},{16,8},{20,12},{24,16},{28,20},{0,24},{4,28},{9,1},{1... | collective-permute-start | bytes 6152 | tf_op jit(solution)/shard_map/ppermute | solution.py:10
  4.0 0.7 collective-permute-start.6
  5.4 0.7 fusion.38
  12.4 1.4 %reshape.25 = bf16[85,4096]{1,0:T(8,128)(2,1)S(1)} reshape(bf16[5,17,4096]{2,1,0:T(8,128)(2,1)} %param.6) | data formatting | bytes 1392640 | tf_op jit(solution)/shard_map/reshape | solution.py:21
  17.1 1.5 %fusion.31 = bf16[85,512]{1,0:T(8,128)(2,1)S(1)} fusion(bf16[85,4096]{1,0:T(8,128)(2,1)S(1)} %reshape.25, s32[512]{0:T(512)S(1)} %collective-permute-done.2), kind=kOutput, calls=%fused_computation.35 | convolution fusion | flops 358656512 | bytes 785408 | tf_op jit(solution)/shard_map/dot_general | solution.py:16
  18.6 1.1 %collective-permute-start.3 = (bf16[85,512]{1,0:T(8,128)(2,1)S(1)}, bf16[85,512]{1,0:T(8,128)(2,1)S(1)}, u32[]{:S(2)}, u32[]{:S(2)}) collective-permute-start(bf16[85,512]{1,0:T(8,128)(2,1)S(1)} %fusion.31), channel_id=1, source_target_pairs={{28,0},{0,4},{4,8},{8,12},{12,16},{16,20},{20,24},{24,28},{29,1},{... | collective-permute-start | bytes 261128 | tf_op jit(solution)/shard_map/ppermute | solution.py:10
  19.7 1.5 %fusion.30 = bf16[85,512]{1,0:T(8,128)(2,1)S(1)} fusion(bf16[85,4096]{1,0:T(8,128)(2,1)S(1)} %reshape.25, s32[512]{0:T(512)S(1)} %collective-permute-done), kind=kOutput, calls=%fused_computation.34 | convolution fusion | flops 358656512 | bytes 785408 | tf_op jit(solution)/shard_map/dot_general | solution.py:16
  21.2 1.6 %collective-permute-start.1 = (bf16[85,512]{1,0:T(8,128)(2,1)S(1)}, bf16[85,512]{1,0:T(8,128)(2,1)S(1)}, u32[]{:S(2)}, u32[]{:S(2)}) collective-permute-start(bf16[85,512]{1,0:T(8,128)(2,1)S(1)} %fusion.30), channel_id=1, source_target_pairs={{24,0},{28,4},{0,8},{4,12},{8,16},{12,20},{16,24},{20,28},{25,1},{... | collective-permute-start | bytes 261128 | tf_op jit(solution)/shard_map/ppermute | solution.py:10
  22.9 1.5 %fusion.34 = bf16[85,512]{1,0:T(8,128)(2,1)S(1)} fusion(bf16[85,4096]{1,0:T(8,128)(2,1)S(1)} %reshape.25, s32[512]{0:T(512)S(1)} %collective-permute-done.4), kind=kOutput, calls=%fused_computation.38 | convolution fusion | flops 358656512 | bytes 785408 | tf_op jit(solution)/shard_map/dot_general | solution.py:16
  24.5 1.5 %fusion.35 = bf16[85,512]{1,0:T(8,128)(2,1)S(1)} fusion(bf16[85,4096]{1,0:T(8,128)(2,1)S(1)} %reshape.25, s32[512]{0:T(512)S(1)} %collective-permute-done.6), kind=kOutput, calls=%fused_computation.39 | convolution fusion | flops 358656512 | bytes 785408 | tf_op jit(solution)/shard_map/dot_general | solution.py:16
  25.9 1.7 %collective-permute-start.7 = (bf16[85,512]{1,0:T(8,128)(2,1)S(1)}, bf16[85,512]{1,0:T(8,128)(2,1)S(1)}, u32[]{:S(2)}, u32[]{:S(2)}) collective-permute-start(bf16[85,512]{1,0:T(8,128)(2,1)S(1)} %fusion.35), channel_id=1, source_target_pairs={{8,0},{12,4},{16,8},{20,12},{24,16},{28,20},{0,24},{4,28},{9,1},{1... | collective-permute-start | bytes 261128 | tf_op jit(solution)/shard_map/ppermute | solution.py:10
  27.7 1.5 %fusion.33 = bf16[5,85,512]{2,1,0:T(8,128)(2,1)S(1)} fusion(bf16[5,85,512]{2,1,0:T(8,128)(2,1)S(1)} %bitcast_dynamic-update-slice_fusion.7, bf16[85,4096]{1,0:T(8,128)(2,1)S(1)} %reshape.25, s32[512]{0:T(512)S(1)} %get-tuple-element.6), kind=kOutput, calls=%fused_computation.37 | convolution fusion | flops 358656512 | bytes 813056 | tf_op jit(solution)/shard_map/dot_general | solution.py:16
  29.2 2.7 %collective-permute-done.7 = bf16[85,512]{1,0:T(8,128)(2,1)S(1)} collective-permute-done((bf16[85,512]{1,0:T(8,128)(2,1)S(1)}, bf16[85,512]{1,0:T(8,128)(2,1)S(1)}, u32[]{:S(2)}, u32[]{:S(2)}) %collective-permute-start.7) | collective-permute-done | bytes 87072 | tf_op jit(solution)/shard_map/ppermute | solution.py:10
  32.0 1.9 %convolution_convert_fusion = bf16[85,2048]{1,0:T(8,128)(2,1)S(1)} fusion(bf16[85,2560]{1,0:T(8,128)(2,1)S(1)} %bitcast_dynamic-update-slice_fusion, bf16[2560,2048]{1,0:T(8,128)(2,1)S(1)} %bitcast.54), kind=kOutput, calls=%fused_computation.26 | convolution fusion | flops 891463680 | bytes 11269120 | tf_op jit(solution)/shard_map/dot_general | solution.py:45
  34.0 4.2 %copy.26 = bf16[5,17,2048]{1,0,2:T(8,128)(2,1)} copy(bf16[5,17,2048]{2,1,0:T(8,128)(2,1)S(1)} %reshape.27) | data formatting | bytes 696320 | tf_op jit(solution)/shard_map/reshape | solution.py:48
  38.2 5.9 %reshape.28 = bf16[4,2,21760]{2,1,0:T(2,128)(2,1)} reshape(bf16[2048,5,17]{2,1,0:T(8,128)(2,1)} %bitcast.55) | data formatting | bytes 696320
  44.2 4.9 %all-to-all-start = ((bf16[4,2,21760]{2,1,0:T(2,128)(2,1)}), bf16[4,2,21760]{2,1,0:T(2,128)(2,1)S(1)}, u32[]{:S(2)}, u32[]{:S(2)}) async-start(bf16[4,2,21760]{2,1,0:T(2,128)(2,1)} %reshape.28), calls=%async_computation | async-start | bytes 696320 | tf_op jit(solution)/shard_map/all_to_all | solution.py:55
  49.6 9.9 %all-to-all-done = bf16[4,2,21760]{2,1,0:T(2,128)(2,1)S(1)} async-done(((bf16[4,2,21760]{2,1,0:T(2,128)(2,1)}), bf16[4,2,21760]{2,1,0:T(2,128)(2,1)S(1)}, u32[]{:S(2)}, u32[]{:S(2)}) %all-to-all-start) | async-done | bytes 348192 | tf_op jit(solution)/shard_map/all_to_all | solution.py:55
  59.5 5.0 %reshape.29 = bf16[2048,5,17]{2,1,0:T(8,128)(2,1)} reshape(bf16[4,2,21760]{2,1,0:T(2,128)(2,1)S(1)} %all-to-all-done) | data formatting | bytes 696320
  64.5 4.2 %copy.35 = bf16[5,17,4,512]{3,2,1,0:T(4,128)(2,1)S(1)} copy(bf16[5,17,4,512]{1,0,3,2:T(8,128)(2,1)} %bitcast.56) | data formatting | bytes 696320 | tf_op jit(solution)/shard_map/all_to_all | solution.py:55
  68.9 0.8 copy.33
  69.7 12.9 %fusion.22 = bf16[5,127,512]{1,0,2:T(8,128)(2,1)S(1)} fusion(bf16[5,68,512]{1,0,2:T(8,128)(2,1)S(1)} %copy.33, f32[127,512]{0,1:T(8,128)S(1)} %copy.32, s32[127,512]{0,1:T(8,128)S(1)} %copy.31, f32[127,512]{0,1:T(8,128)S(1)} %copy.30, s32[127,512]{0,1:T(8,128)S(1)} %copy.29), kind=kOutput, calls=%fused_computation.28 | convolution fusion | flops 287731200 | bytes 2038784 | tf_op jit(solution)/shard_map/jlc,flc->fjc/dot_general | solution.py:58
  82.6 1.4 %copy.34 = bf16[5,127,512]{2,1,0:T(8,128)(2,1)} copy(bf16[5,127,512]{1,0,2:T(8,128)(2,1)S(1)} %fusion.22) | data formatting | bytes 1300480 | tf_op jit(solution)/shard_map/convert_element_type | solution.py:59
  (41 shorter events, 2.5 us)
Async XLA Ops:
  1.5 15.6 %collective-permute-start.2 = (s32[512]{0:T(512)S(1)}, s32[512]{0:T(512)S(1)}, u32[]{:S(2)}, u32[]{:S(2)}) collective-permute-start(s32[512]{0:T(512)S(1)} %get-tuple-element.7), channel_id=1, source_target_pairs={{4,0},{8,4},{12,8},{16,12},{20,16},{24,20},{28,24},{0,28},{5,1},{9... | collective-permute-start | bytes 6152 | tf_op jit(solution)/shard_map/ppermute | solution.py:10
  1.6 18.2 %collective-permute-start = (s32[512]{0:T(512)S(1)}, s32[512]{0:T(512)S(1)}, u32[]{:S(2)}, u32[]{:S(2)}) collective-permute-start(s32[512]{0:T(512)S(1)} %get-tuple-element.8), channel_id=1, source_target_pairs={{8,0},{12,4},{16,8},{20,12},{24,16},{28,20},{0,24},{4,28},{9,1},{1... | collective-permute-start | bytes 6152 | tf_op jit(solution)/shard_map/ppermute | solution.py:10
  4.0 18.9 %collective-permute-start.4 = (s32[512]{0:T(512)S(1)}, s32[512]{0:T(512)S(1)}, u32[]{:S(2)}, u32[]{:S(2)}) collective-permute-start(s32[512]{0:T(512)S(1)} %get-tuple-element.9), channel_id=1, source_target_pairs={{28,0},{0,4},{4,8},{8,12},{12,16},{16,20},{20,24},{24,28},{29,1},{... | collective-permute-start | bytes 6152 | tf_op jit(solution)/shard_map/ppermute | solution.py:10
  4.0 20.5 %collective-permute-start.6 = (s32[512]{0:T(512)S(1)}, s32[512]{0:T(512)S(1)}, u32[]{:S(2)}, u32[]{:S(2)}) collective-permute-start(s32[512]{0:T(512)S(1)} %get-tuple-element.5), channel_id=1, source_target_pairs={{24,0},{28,4},{0,8},{4,12},{8,16},{12,20},{16,24},{20,28},{25,1},{... | collective-permute-start | bytes 6152 | tf_op jit(solution)/shard_map/ppermute | solution.py:10
  17.1 14.9 %slice-start = ((s8[10485760]{0:T(1024)(128)(4,1)}), s8[4194304]{0:T(1024)(128)(4,1)S(1)}, s32[]{:S(2)}) async-start(s8[10485760]{0:T(1024)(128)(4,1)} %bitcast.52), calls=%async_computation.1 | async-start | bytes 8388608
  18.6 13.4 %slice-start.1 = ((s8[10485760]{0:T(1024)(128)(4,1)}), s8[4194304]{0:T(1024)(128)(4,1)S(1)}, s32[]{:S(2)}) async-start(s8[10485760]{0:T(1024)(128)(4,1)} %bitcast.52), calls=%async_computation.2 | async-start | bytes 8388608
  18.6 9.1 %collective-permute-start.3 = (bf16[85,512]{1,0:T(8,128)(2,1)S(1)}, bf16[85,512]{1,0:T(8,128)(2,1)S(1)}, u32[]{:S(2)}, u32[]{:S(2)}) collective-permute-start(bf16[85,512]{1,0:T(8,128)(2,1)S(1)} %fusion.31), channel_id=1, source_target_pairs={{28,0},{0,4},{4,8},{8,12},{12,16},{16,20},{20,24},{24,28},{29,1},{... | collective-permute-start | bytes 261128 | tf_op jit(solution)/shard_map/ppermute | solution.py:10
  21.2 6.5 %collective-permute-start.1 = (bf16[85,512]{1,0:T(8,128)(2,1)S(1)}, bf16[85,512]{1,0:T(8,128)(2,1)S(1)}, u32[]{:S(2)}, u32[]{:S(2)}) collective-permute-start(bf16[85,512]{1,0:T(8,128)(2,1)S(1)} %fusion.30), channel_id=1, source_target_pairs={{24,0},{28,4},{0,8},{4,12},{8,16},{12,20},{16,24},{20,28},{25,1},{... | collective-permute-start | bytes 261128 | tf_op jit(solution)/shard_map/ppermute | solution.py:10
  24.3 7.7 %slice-start.2 = ((s8[10485760]{0:T(1024)(128)(4,1)}), s8[2097152]{0:T(1024)(128)(4,1)S(1)}, s32[]{:S(2)}) async-start(s8[10485760]{0:T(1024)(128)(4,1)} %bitcast.52), calls=%async_computation.3 | async-start | bytes 4194304
  24.3 4.8 %collective-permute-start.5 = (bf16[85,512]{1,0:T(8,128)(2,1)S(1)}, bf16[85,512]{1,0:T(8,128)(2,1)S(1)}, u32[]{:S(2)}, u32[]{:S(2)}) collective-permute-start(bf16[85,512]{1,0:T(8,128)(2,1)S(1)} %fusion.34), channel_id=1, source_target_pairs={{4,0},{8,4},{12,8},{16,12},{20,16},{24,20},{28,24},{0,28},{5,1},{9... | collective-permute-start | bytes 261128 | tf_op jit(solution)/shard_map/ppermute | solution.py:10
  25.9 5.9 %collective-permute-start.7 = (bf16[85,512]{1,0:T(8,128)(2,1)S(1)}, bf16[85,512]{1,0:T(8,128)(2,1)S(1)}, u32[]{:S(2)}, u32[]{:S(2)}) collective-permute-start(bf16[85,512]{1,0:T(8,128)(2,1)S(1)} %fusion.35), channel_id=1, source_target_pairs={{8,0},{12,4},{16,8},{20,12},{24,16},{28,20},{0,24},{4,28},{9,1},{1... | collective-permute-start | bytes 261128 | tf_op jit(solution)/shard_map/ppermute | solution.py:10
  33.9 15.1 %copy-start = (f32[127,512]{1,0:T(8,128)S(1)}, f32[127,512]{1,0:T(8,128)}, u32[]{:S(2)}) copy-start(f32[127,512]{1,0:T(8,128)} %param.11) | copy-start | bytes 780292
  33.9 15.4 %copy-start.1 = (s32[127,512]{1,0:T(8,128)S(1)}, s32[127,512]{1,0:T(8,128)}, u32[]{:S(2)}) copy-start(s32[127,512]{1,0:T(8,128)} %param.10) | copy-start | bytes 780292
  44.2 15.4 %all-to-all-start = ((bf16[4,2,21760]{2,1,0:T(2,128)(2,1)}), bf16[4,2,21760]{2,1,0:T(2,128)(2,1)S(1)}, u32[]{:S(2)}, u32[]{:S(2)}) async-start(bf16[4,2,21760]{2,1,0:T(2,128)(2,1)} %reshape.28), calls=%async_computation | async-start | bytes 696320 | tf_op jit(solution)/shard_map/all_to_all | solution.py:55
where the time goes:
time: 84.6 us; the launch traced here: 84 us
  local copies, waits for them, and re-layouts  24.5 us (29%)
  matrix products  22.2 us (26%)
  starting transfers between devices  12.7 us (15%)
  waiting for transfers between devices  12.5 us (15%)
  between operations  9.9 us (12%)
  other arithmetic  2.19 us (3%)
    dot_general x1, matrix products, local(): jnp.einsum('jlc,flc->fjc', interp, widened, precision=lax.Precision.HIGHEST)  12.9 us
    unnamed x21, local copies, waits for them, and re-layouts  11.2 us
    all_to_all x1, waiting for transfers between devices, local(): lax.all_to_all(horizontal, 'lev', split_axis=2, concat_axis=1, tiled=True)  9.87 us
    ppermute x8, starting transfers between devices, shifted(): return lax.ppermute(block, axis, route)  7.8 us
    dot_general x5, matrix products, select_cells(): jnp.dot(tile, picker, preferred_element_type=jnp.float32)  7.4 us
    all_to_all x4, local copies, waits for them, and re-layouts, local(): lax.all_to_all(horizontal, 'lev', split_axis=2, concat_axis=1, tiled=True)  5.19 us
    all_to_all x1, starting transfers between devices, local(): lax.all_to_all(horizontal, 'lev', split_axis=2, concat_axis=1, tiled=True)  4.88 us
    reshape x2, local copies, waits for them, and re-layouts, local(): horizontal = horizontal.reshape(fields, level_slab, blocks.shape[2])  4.33 us
  transfers between devices with their start and end apart: 9, of which 2 were waited for; matrix products, arithmetic and copies ran while one was open for 13% of the time, Pallas kernels for 0%

commit v1 on v0

--- a/solution.py
+++ b/solution.py
@@ -52,9 +52,10 @@
     upper_hit = level_ids == bracket[:, None, :] + 1
     upper_share = fraction[:, None, :]
     interp = jnp.where(lower_hit, 1.0 - upper_share, 0.0) + jnp.where(upper_hit, upper_share, 0.0)
-    widened = lax.all_to_all(horizontal, "lev", split_axis=2, concat_axis=1, tiled=True).astype(
-        jnp.float32
-    )
+    widened = jnp.concatenate(
+        lax.all_to_all(jnp.stack(jnp.split(horizontal, lax.axis_size("lev"), axis=2)), "lev", 0, 0),
+        axis=1,
+    ).astype(jnp.float32)
     mixed = jnp.einsum("jlc,flc->fjc", interp, widened, precision=lax.Precision.HIGHEST)
     return mixed.astype(jnp.bfloat16)
 

time: 84.6 us -> 68.7 us (0.81)
  local copies, waits for them, and re-layouts: 24.5 us -> 5.21 us
  waiting for transfers between devices: 12.5 us -> 14.9 us
  other arithmetic: 2.19 us -> 3.05 us
    unnamed x21 -> x19, local copies, waits for them, and re-layouts: 11.2 us -> 0.37 us
    all_to_all x4 -> x0, local copies, waits for them, and re-layouts: 5.19 us -> none  [local(): lax.all_to_all(horizontal, 'lev', split_axis=2, concat_axis=1, tiled=True)]
    reshape x2 -> x1, local copies, waits for them, and re-layouts: 4.33 us -> 0.12 us  [local(): horizontal = horizontal.reshape(fields, level_slab, blocks.shape[2])]
    all_to_all x1, waiting for transfers between devices: 9.87 us -> 11.7 us  [local(): lax.all_to_all(jnp.stack(jnp.split(horizontal, lax.axis_size('lev'), axis...]
    reshape x0 -> x3, local copies, waits for them, and re-layouts: none -> 0.92 us  [local(): jnp.concatenate(lax.all_to_all(jnp.stack(jnp.split(horizontal, lax.axis_s...]
    another operation x0 -> x1, other arithmetic: none -> 0.86 us  [local(): jnp.stack(jnp.split(horizontal, lax.axis_size('lev'), axis=2))]
  transfers between devices with their start and end apart: 9 -> 9, of which waited for: 2 -> 2; matrix products, arithmetic and copies ran while one was open for 13% -> 16% of each run, Pallas kernels for 0% -> 0%
where the time goes in v1:
time: 68.7 us; the launch traced here: 67.3 us
  matrix products  22.2 us (32%)
  waiting for transfers between devices  14.9 us (22%)
  starting transfers between devices  12.3 us (18%)
  between operations  9.73 us (14%)
  local copies, waits for them, and re-layouts  5.21 us (8%)
  other arithmetic  3.05 us (4%)
    dot_general x1, matrix products, local(): jnp.einsum('jlc,flc->fjc', interp, widened, precision=lax.Precision.HIGHEST)  12.9 us
    all_to_all x1, waiting for transfers between devices, local(): lax.all_to_all(jnp.stack(jnp.split(horizontal, lax.axis_size('lev'), axis...  11.7 us
    ppermute x8, starting transfers between devices, shifted(): return lax.ppermute(block, axis, route)  7.42 us
    dot_general x5, matrix products, select_cells(): jnp.dot(tile, picker, preferred_element_type=jnp.float32)  7.4 us
    all_to_all x1, starting transfers between devices, local(): lax.all_to_all(jnp.stack(jnp.split(horizontal, lax.axis_size('lev'), axis...  4.88 us
    ppermute x8, waiting for transfers between devices, shifted(): return lax.ppermute(block, axis, route)  3.13 us
    dot_general x1, matrix products, local(): jnp.dot(chosen, weights_flat, preferred_element_type=jnp.float32)  1.85 us
    reshape x1, local copies, waits for them, and re-layouts, local(): stacked = source_state.reshape(fields * level_slab, tile_cells)  1.45 us
  transfers between devices with their start and end apart: 9, of which 2 were waited for; matrix products, arithmetic and copies ran while one was open for 16% of the time, Pallas kernels for 0%

profile of v1, /device:TPU:2, one launch (start us, length us, event | category | flops | bytes accessed | tf_op | source)
XLA Modules:
  0.0 67.3 jit_solution(3624340371518936632)
XLA Ops:
  0.0 0.7 broadcast_compare_fusion.1
  0.7 0.8 %select_reduce_fusion = (s32[512]{0:T(512)S(1)}, s32[512]{0:T(512)S(1)}, s32[512]{0:T(512)S(1)}, s32[512]{0:T(512)S(1)}, s32[512]{0:T(512)S(1)}) fusion(s32[5,512]{1,0:T(8,128)} %param.8, pred[5]{0:T(512)(128)(4,1)S(1)} %get-tuple-element.23, pred[5]{0:T(512)(128)(4,1)S(1)} %get-tuple-element.20, pred[5]{0:T(512)(128)(4,1)S(1)} %get-tuple-element.21, ...), kind=kLoop, calls=%fused_computation.56 | loop fusion | flops 23040 | bytes 20505 | tf_op jit(solution)/shard_map/reduce_sum | solution.py:31
  1.5 1.5 %collective-permute-start.6 = (s32[512]{0:T(512)S(1)}, s32[512]{0:T(512)S(1)}, u32[]{:S(2)}, u32[]{:S(2)}) collective-permute-start(s32[512]{0:T(512)S(1)} %get-tuple-element.5), channel_id=1, source_target_pairs={{24,0},{28,4},{0,8},{4,12},{8,16},{12,20},{16,24},{20,28},{25,1},{... | collective-permute-start | bytes 6152 | tf_op jit(solution)/shard_map/ppermute | solution.py:10
  3.0 1.0 %collective-permute-start = (s32[512]{0:T(512)S(1)}, s32[512]{0:T(512)S(1)}, u32[]{:S(2)}, u32[]{:S(2)}) collective-permute-start(s32[512]{0:T(512)S(1)} %get-tuple-element.8), channel_id=1, source_target_pairs={{8,0},{12,4},{16,8},{20,12},{24,16},{28,20},{0,24},{4,28},{9,1},{1... | collective-permute-start | bytes 6152 | tf_op jit(solution)/shard_map/ppermute | solution.py:10
  4.0 0.7 and_select_fusion
  4.7 0.7 fusion.38
  11.7 1.4 %reshape.31 = bf16[85,4096]{1,0:T(8,128)(2,1)S(1)} reshape(bf16[5,17,4096]{2,1,0:T(8,128)(2,1)} %param.6) | data formatting | bytes 1392640 | tf_op jit(solution)/shard_map/reshape | solution.py:21
  16.3 1.5 %fusion.30 = bf16[85,512]{1,0:T(8,128)(2,1)S(1)} fusion(bf16[85,4096]{1,0:T(8,128)(2,1)S(1)} %reshape.31, s32[512]{0:T(512)S(1)} %collective-permute-done), kind=kOutput, calls=%fused_computation.34 | convolution fusion | flops 358656512 | bytes 785408 | tf_op jit(solution)/shard_map/dot_general | solution.py:16
  17.8 2.2 %collective-permute-start.1 = (bf16[85,512]{1,0:T(8,128)(2,1)S(1)}, bf16[85,512]{1,0:T(8,128)(2,1)S(1)}, u32[]{:S(2)}, u32[]{:S(2)}) collective-permute-start(bf16[85,512]{1,0:T(8,128)(2,1)S(1)} %fusion.30), channel_id=1, source_target_pairs={{24,0},{28,4},{0,8},{4,12},{8,16},{12,20},{16,24},{20,28},{25,1},{... | collective-permute-start | bytes 261128 | tf_op jit(solution)/shard_map/ppermute | solution.py:10
  20.0 1.5 %fusion.31 = bf16[85,512]{1,0:T(8,128)(2,1)S(1)} fusion(bf16[85,4096]{1,0:T(8,128)(2,1)S(1)} %reshape.31, s32[512]{0:T(512)S(1)} %collective-permute-done.2), kind=kOutput, calls=%fused_computation.35 | convolution fusion | flops 358656512 | bytes 785408 | tf_op jit(solution)/shard_map/dot_general | solution.py:16
  21.5 0.8 %collective-permute-start.3 = (bf16[85,512]{1,0:T(8,128)(2,1)S(1)}, bf16[85,512]{1,0:T(8,128)(2,1)S(1)}, u32[]{:S(2)}, u32[]{:S(2)}) collective-permute-start(bf16[85,512]{1,0:T(8,128)(2,1)S(1)} %fusion.31), channel_id=1, source_target_pairs={{28,0},{0,4},{4,8},{8,12},{12,16},{16,20},{20,24},{24,28},{29,1},{... | collective-permute-start | bytes 261128 | tf_op jit(solution)/shard_map/ppermute | solution.py:10
  22.3 1.5 %fusion.34 = bf16[85,512]{1,0:T(8,128)(2,1)S(1)} fusion(bf16[85,4096]{1,0:T(8,128)(2,1)S(1)} %reshape.31, s32[512]{0:T(512)S(1)} %collective-permute-done.4), kind=kOutput, calls=%fused_computation.38 | convolution fusion | flops 358656512 | bytes 785408 | tf_op jit(solution)/shard_map/dot_general | solution.py:16
  23.8 1.0 %collective-permute-start.5 = (bf16[85,512]{1,0:T(8,128)(2,1)S(1)}, bf16[85,512]{1,0:T(8,128)(2,1)S(1)}, u32[]{:S(2)}, u32[]{:S(2)}) collective-permute-start(bf16[85,512]{1,0:T(8,128)(2,1)S(1)} %fusion.34), channel_id=1, source_target_pairs={{4,0},{8,4},{12,8},{16,12},{20,16},{24,20},{28,24},{0,28},{5,1},{9... | collective-permute-start | bytes 261128 | tf_op jit(solution)/shard_map/ppermute | solution.py:10
  24.8 1.5 %fusion.35 = bf16[85,512]{1,0:T(8,128)(2,1)S(1)} fusion(bf16[85,4096]{1,0:T(8,128)(2,1)S(1)} %reshape.31, s32[512]{0:T(512)S(1)} %collective-permute-done.6), kind=kOutput, calls=%fused_computation.39 | convolution fusion | flops 358656512 | bytes 785408 | tf_op jit(solution)/shard_map/dot_general | solution.py:16
  26.3 0.8 %collective-permute-start.7 = (bf16[85,512]{1,0:T(8,128)(2,1)S(1)}, bf16[85,512]{1,0:T(8,128)(2,1)S(1)}, u32[]{:S(2)}, u32[]{:S(2)}) collective-permute-start(bf16[85,512]{1,0:T(8,128)(2,1)S(1)} %fusion.35), channel_id=1, source_target_pairs={{8,0},{12,4},{16,8},{20,12},{24,16},{28,20},{0,24},{4,28},{9,1},{1... | collective-permute-start | bytes 261128 | tf_op jit(solution)/shard_map/ppermute | solution.py:10
  27.2 1.5 %fusion.33 = bf16[5,85,512]{2,1,0:T(8,128)(2,1)S(1)} fusion(bf16[5,85,512]{2,1,0:T(8,128)(2,1)S(1)} %bitcast_dynamic-update-slice_fusion.7, bf16[85,4096]{1,0:T(8,128)(2,1)S(1)} %reshape.31, s32[512]{0:T(512)S(1)} %get-tuple-element.6), kind=kOutput, calls=%fused_computation.37 | convolution fusion | flops 358656512 | bytes 813056 | tf_op jit(solution)/shard_map/dot_general | solution.py:16
  28.7 3.1 %collective-permute-done.7 = bf16[85,512]{1,0:T(8,128)(2,1)S(1)} collective-permute-done((bf16[85,512]{1,0:T(8,128)(2,1)S(1)}, bf16[85,512]{1,0:T(8,128)(2,1)S(1)}, u32[]{:S(2)}, u32[]{:S(2)}) %collective-permute-start.7) | collective-permute-done | bytes 87072 | tf_op jit(solution)/shard_map/ppermute | solution.py:10
  32.0 1.9 %convolution_convert_fusion = bf16[85,2048]{1,0:T(8,128)(2,1)S(1)} fusion(bf16[85,2560]{1,0:T(8,128)(2,1)S(1)} %bitcast_dynamic-update-slice_fusion, bf16[2560,2048]{1,0:T(8,128)(2,1)S(1)} %bitcast.59), kind=kOutput, calls=%fused_computation.26 | convolution fusion | flops 891463680 | bytes 11269120 | tf_op jit(solution)/shard_map/dot_general | solution.py:45
  34.0 0.9 %pad_maximum_fusion = bf16[4,5,17,512]{3,2,1,0:T(8,128)(2,1)} fusion(bf16[1,5,17,512]{3,2,1,0:T(8,128)(2,1)S(1)} %get-tuple-element.11, bf16[1,5,17,512]{3,2,1,0:T(8,128)(2,1)S(1)} %get-tuple-element.12, bf16[1,5,17,512]{3,2,1,0:T(8,128)(2,1)S(1)} %get-tuple-element.13, bf16[1,5,17,512]{3,2,1,0:T(8,128)(2,1)S(1)} %get-tuple-element.10), kind=kLoop, calls=%fused_computation.40 | loop fusion | flops 522240 | bytes 696320 | tf_op jit(solution)/shard_map/stack | solution.py:56
  34.8 4.9 %all-to-all-start = ((bf16[4,5,17,512]{3,2,1,0:T(8,128)(2,1)}), bf16[4,5,17,512]{3,2,1,0:T(8,128)(2,1)S(1)}, u32[]{:S(2)}, u32[]{:S(2)}) async-start(bf16[4,5,17,512]{3,2,1,0:T(8,128)(2,1)} %pad_maximum_fusion), calls=%async_computation | async-start | bytes 983040 | tf_op jit(solution)/shard_map/all_to_all | solution.py:56
  40.3 11.7 %all-to-all-done = bf16[4,5,17,512]{3,2,1,0:T(8,128)(2,1)S(1)} async-done(((bf16[4,5,17,512]{3,2,1,0:T(8,128)(2,1)}), bf16[4,5,17,512]{3,2,1,0:T(8,128)(2,1)S(1)}, u32[]{:S(2)}, u32[]{:S(2)}) %all-to-all-start) | async-done | bytes 348192 | tf_op jit(solution)/shard_map/all_to_all | solution.py:56
  52.3 0.8 %copy.27 = bf16[5,68,512]{1,0,2:T(8,128)(2,1)S(1)} copy(bf16[5,68,512]{2,1,0:T(8,128)(2,1)S(1)} %reshape.35) | data formatting | bytes 696320 | tf_op jit(solution)/shard_map/reshape | solution.py:55
  53.0 12.9 %fusion.22 = bf16[5,127,512]{1,0,2:T(8,128)(2,1)S(1)} fusion(bf16[5,68,512]{1,0,2:T(8,128)(2,1)S(1)} %copy.27, f32[127,512]{0,1:T(8,128)S(1)} %copy.26, s32[127,512]{0,1:T(8,128)S(1)} %copy.25, f32[127,512]{0,1:T(8,128)S(1)} %copy.24, s32[127,512]{0,1:T(8,128)S(1)} %copy.23), kind=kOutput, calls=%fused_computation.28 | convolution fusion | flops 287731200 | bytes 2038784 | tf_op jit(solution)/shard_map/jlc,flc->fjc/dot_general | solution.py:59
  66.0 1.4 %copy.28 = bf16[5,127,512]{2,1,0:T(8,128)(2,1)} copy(bf16[5,127,512]{1,0,2:T(8,128)(2,1)S(1)} %fusion.22) | data formatting | bytes 1300480 | tf_op jit(solution)/shard_map/convert_element_type | solution.py:60
  (39 shorter events, 1.0 us)
Async XLA Ops:
  1.5 23.3 %collective-permute-start.6 = (s32[512]{0:T(512)S(1)}, s32[512]{0:T(512)S(1)}, u32[]{:S(2)}, u32[]{:S(2)}) collective-permute-start(s32[512]{0:T(512)S(1)} %get-tuple-element.5), channel_id=1, source_target_pairs={{24,0},{28,4},{0,8},{4,12},{8,16},{12,20},{16,24},{20,28},{25,1},{... | collective-permute-start | bytes 6152 | tf_op jit(solution)/shard_map/ppermute | solution.py:10
  3.0 17.0 %collective-permute-start.2 = (s32[512]{0:T(512)S(1)}, s32[512]{0:T(512)S(1)}, u32[]{:S(2)}, u32[]{:S(2)}) collective-permute-start(s32[512]{0:T(512)S(1)} %get-tuple-element.7), channel_id=1, source_target_pairs={{4,0},{8,4},{12,8},{16,12},{20,16},{24,20},{28,24},{0,28},{5,1},{9... | collective-permute-start | bytes 6152 | tf_op jit(solution)/shard_map/ppermute | solution.py:10
  3.0 13.2 %collective-permute-start = (s32[512]{0:T(512)S(1)}, s32[512]{0:T(512)S(1)}, u32[]{:S(2)}, u32[]{:S(2)}) collective-permute-start(s32[512]{0:T(512)S(1)} %get-tuple-element.8), channel_id=1, source_target_pairs={{8,0},{12,4},{16,8},{20,12},{24,16},{28,20},{0,24},{4,28},{9,1},{1... | collective-permute-start | bytes 6152 | tf_op jit(solution)/shard_map/ppermute | solution.py:10
  4.0 18.3 %collective-permute-start.4 = (s32[512]{0:T(512)S(1)}, s32[512]{0:T(512)S(1)}, u32[]{:S(2)}, u32[]{:S(2)}) collective-permute-start(s32[512]{0:T(512)S(1)} %get-tuple-element.9), channel_id=1, source_target_pairs={{28,0},{0,4},{4,8},{8,12},{12,16},{16,20},{20,24},{24,28},{29,1},{... | collective-permute-start | bytes 6152 | tf_op jit(solution)/shard_map/ppermute | solution.py:10
  16.3 15.6 %slice-start = ((s8[10485760]{0:T(1024)(128)(4,1)}), s8[4194304]{0:T(1024)(128)(4,1)S(1)}, s32[]{:S(2)}) async-start(s8[10485760]{0:T(1024)(128)(4,1)} %bitcast.57), calls=%async_computation.1 | async-start | bytes 8388608
  17.8 14.1 %slice-start.1 = ((s8[10485760]{0:T(1024)(128)(4,1)}), s8[4194304]{0:T(1024)(128)(4,1)S(1)}, s32[]{:S(2)}) async-start(s8[10485760]{0:T(1024)(128)(4,1)} %bitcast.57), calls=%async_computation.2 | async-start | bytes 8388608
  17.8 9.3 %collective-permute-start.1 = (bf16[85,512]{1,0:T(8,128)(2,1)S(1)}, bf16[85,512]{1,0:T(8,128)(2,1)S(1)}, u32[]{:S(2)}, u32[]{:S(2)}) collective-permute-start(bf16[85,512]{1,0:T(8,128)(2,1)S(1)} %fusion.30), channel_id=1, source_target_pairs={{24,0},{28,4},{0,8},{4,12},{8,16},{12,20},{16,24},{20,28},{25,1},{... | collective-permute-start | bytes 261128 | tf_op jit(solution)/shard_map/ppermute | solution.py:10
  21.5 5.7 %collective-permute-start.3 = (bf16[85,512]{1,0:T(8,128)(2,1)S(1)}, bf16[85,512]{1,0:T(8,128)(2,1)S(1)}, u32[]{:S(2)}, u32[]{:S(2)}) collective-permute-start(bf16[85,512]{1,0:T(8,128)(2,1)S(1)} %fusion.31), channel_id=1, source_target_pairs={{28,0},{0,4},{4,8},{8,12},{12,16},{16,20},{20,24},{24,28},{29,1},{... | collective-permute-start | bytes 261128 | tf_op jit(solution)/shard_map/ppermute | solution.py:10
  23.8 8.1 %slice-start.2 = ((s8[10485760]{0:T(1024)(128)(4,1)}), s8[2097152]{0:T(1024)(128)(4,1)S(1)}, s32[]{:S(2)}) async-start(s8[10485760]{0:T(1024)(128)(4,1)} %bitcast.57), calls=%async_computation.3 | async-start | bytes 4194304
  23.8 4.8 %collective-permute-start.5 = (bf16[85,512]{1,0:T(8,128)(2,1)S(1)}, bf16[85,512]{1,0:T(8,128)(2,1)S(1)}, u32[]{:S(2)}, u32[]{:S(2)}) collective-permute-start(bf16[85,512]{1,0:T(8,128)(2,1)S(1)} %fusion.34), channel_id=1, source_target_pairs={{4,0},{8,4},{12,8},{16,12},{20,16},{24,20},{28,24},{0,28},{5,1},{9... | collective-permute-start | bytes 261128 | tf_op jit(solution)/shard_map/ppermute | solution.py:10
  26.3 5.5 %collective-permute-start.7 = (bf16[85,512]{1,0:T(8,128)(2,1)S(1)}, bf16[85,512]{1,0:T(8,128)(2,1)S(1)}, u32[]{:S(2)}, u32[]{:S(2)}) collective-permute-start(bf16[85,512]{1,0:T(8,128)(2,1)S(1)} %fusion.35), channel_id=1, source_target_pairs={{8,0},{12,4},{16,8},{20,12},{24,16},{28,20},{0,24},{4,28},{9,1},{1... | collective-permute-start | bytes 261128 | tf_op jit(solution)/shard_map/ppermute | solution.py:10
  31.9 7.8 %copy-start = (s32[127,512]{1,0:T(8,128)S(1)}, s32[127,512]{1,0:T(8,128)}, u32[]{:S(2)}) copy-start(s32[127,512]{1,0:T(8,128)} %param.10) | copy-start | bytes 780292
  31.9 8.1 %copy-start.1 = (f32[127,512]{1,0:T(8,128)S(1)}, f32[127,512]{1,0:T(8,128)}, u32[]{:S(2)}) copy-start(f32[127,512]{1,0:T(8,128)} %param.11) | copy-start | bytes 780292
  34.8 17.2 %all-to-all-start = ((bf16[4,5,17,512]{3,2,1,0:T(8,128)(2,1)}), bf16[4,5,17,512]{3,2,1,0:T(8,128)(2,1)S(1)}, u32[]{:S(2)}, u32[]{:S(2)}) async-start(bf16[4,5,17,512]{3,2,1,0:T(8,128)(2,1)} %pad_maximum_fusion), calls=%async_computation | async-start | bytes 983040 | tf_op jit(solution)/shard_map/all_to_all | solution.py:56
